TPU v7x, 32 devices: a whole 2x2x4 slice. The times are simulated.
32 devices in a mesh: dp: 8 (over z, y), fsdp: 4 (over x, core).
Axes of the slice: x: 2, y: 2, z: 4, core: 2. Of those that a mesh axis runs over, the one named last changes fastest.
Arguments:
- tokens: bfloat16 [16384, 768], P(('dp', 'fsdp')), may hold values from -6 to 6
- valid_mask: int32 [16384], P(('dp', 'fsdp')), may hold values 0 or 1
- target: bfloat16 [16384, 768], P(('dp', 'fsdp')), may hold values from -8 to 8
- params: float32 [55552, 128], P(('dp', 'fsdp')), may hold values from -4 to 4, as said below
- first_moment: float32 [55552, 128], P(('dp', 'fsdp')), may hold values from -1 to 1, as said below
- second_moment: float32 [55552, 128], P(('dp', 'fsdp')), may hold values from 0 to 1, as said below
Outputs:
- activations: bfloat16 [16384, 768], P(('dp', 'fsdp'))
- loss: float32 [], replicated
- input_grad: float32 [16384, 768], P(('dp', 'fsdp'))
- new_params: float32 [55552, 128], P(('dp', 'fsdp'))
- new_first: float32 [55552, 128], P(('dp', 'fsdp'))
- new_second: float32 [55552, 128], P(('dp', 'fsdp'))
Inputs may be any that keep to these rules, and one draw needn't show every extreme that they name: `params`: entries beyond 7087104 in row order are zero. `first_moment`: entries beyond 7087104 in row order are zero. `second_moment`: entries beyond 7087104 in row order are zero.
All inputs are finite; a program needn't handle non-finite values. No bound on the sum of `valid_mask` on one device may be relied on, other than what follows from the above.
Results may differ from a plain program's by a relative error of at most 0.012.
The roundings to bfloat16 on the way count: a program that leaves them out, or rounds other values in their place, can miss the bound.
Values may be sent and summed in bfloat16 or wider, within the bound.
A program may use at most 128 MiB of HBM per device.

v0:
```python
import functools
import math

import jax
import jax.numpy as jnp
from jax import lax
from jax.experimental import pallas as pl
from jax.experimental.pallas import tpu as pltpu
from jax.sharding import PartitionSpec as P

D = 768
HEADS = 12
HEAD = 64
FF = 3072
FRAMES = 16
STEP = 10


norm_epsilon = 1e-06
adam_epsilon = 1e-08
beta_one = 0.9
beta_two = 0.999
learn_rate = 0.1
weight_decay = 0.05

def unpack(tiled):
    flat = tiled.reshape(-1)
    layout = [(D, 3 * D), (D, D), (D, FF), (D, FF)]
    pieces = []
    offset = 0
    for height, breadth in layout:
        pieces.append(flat[offset : offset + height * breadth].reshape(height, breadth))
        offset = offset + height * breadth
    for length in [D] * 8 + [FF]:
        pieces.append(flat[offset : offset + length].astype(jnp.float32))
        offset = offset + length
    return pieces


def collect(shard):
    lowered = shard.astype(jnp.bfloat16)
    whole = lax.all_gather(lowered, ("dp", "fsdp"), axis=0, tiled=True)
    return whole


def reduce_rows(full):
    summed = lax.psum_scatter(full, ("dp", "fsdp"), scatter_dimension=0, tiled=True)
    return summed


MESH = pl.DeviceIdType.MESH
NA, NB, NX = 4, 2, 2
ORDERS = ((0, 1, 2), (0, 2, 1), (1, 2, 0))


def coords():
    dp = lax.axis_index("dp")
    fs = lax.axis_index("fsdp")
    return (dp // NB, dp % NB, fs // 2), fs % 2


def device(pos, core):
    return (pos[0] * NB + pos[1], pos[2] * 2 + core)


def flat(pos, core):
    return ((pos[0] * NB + pos[1]) * NX + pos[2]) * 2 + core


def steps():
    out = []
    for da in range(-(NA - 1), NA):
        for db in range(2):
            for dx in range(2):
                out.append((abs(da) + db + dx, (da, db, dx)))
    out.sort(key=lambda t: t[0])
    return [r for _, r in out]


def children(rel, order, pos):
    last = -1
    for i, d in enumerate(order):
        if rel[d] != 0:
            last = i
    res = []

    def line(up):
        a = pos[0]
        if up:
            return (a + 1 < NA, (a + 1, pos[1], pos[2]), 0)
        return (a - 1 >= 0, (a - 1, pos[1], pos[2]), 1)

    def flip(d):
        p = list(pos)
        p[d] = 1 - p[d]
        return (None, tuple(p), 1 + d)

    if last >= 0 and order[last] == 0:
        res.append(line(rel[0] < 0))
    for i in range(last + 1, 3):
        d = order[i]
        if d == 0:
            res.append(line(True))
            res.append(line(False))
        else:
            res.append(flip(d))
    return res


def source_of(rel, pos):
    a = pos[0] + rel[0]
    valid = None
    if rel[0] > 0:
        valid = a < NA
    if rel[0] < 0:
        valid = a >= 0
    return valid, (a, (pos[1] + rel[1]) % 2, (pos[2] + rel[2]) % 2)


def when(cond, fn):
    if cond is None:
        fn()
    else:
        pl.when(cond)(fn)


def both(a, b):
    if a is None:
        return b
    if b is None:
        return a
    return jnp.logical_and(a, b)


def split_rows(rows, shares):
    tiles = rows // 16
    first = int(round(tiles * shares))
    return ((0, first * 16), (first * 16, first * 16), (2 * first * 16, rows - 2 * first * 16))


F32, BF16 = jnp.float32, jnp.bfloat16
SHARE = 0.389


def greet(pos, core):
    sem = pltpu.get_barrier_semaphore()
    a, b, x = pos
    fixed = [device(pos, 1 - core), device((a, 1 - b, x), core), device((a, b, 1 - x), core),
             device(((a + 2) % NA, b, x), core)]
    for d in fixed:
        pl.semaphore_signal(sem, inc=1, device_id=d, device_id_type=MESH)
    up, down = a + 1 < NA, a - 1 >= 0
    when(up, lambda: pl.semaphore_signal(sem, inc=1, device_id=device((a + 1, b, x), core), device_id_type=MESH))
    when(down, lambda: pl.semaphore_signal(sem, inc=1, device_id=device((a - 1, b, x), core), device_id_type=MESH))
    pl.semaphore_wait(sem, len(fixed) + up.astype(jnp.int32) + down.astype(jnp.int32))


class Total:
    def __init__(self, pos, core, buf, send, recv):
        a, b, x = pos
        flip = a + 1 - 2 * (a % 2)
        partners = [device(pos, 1 - core), device((a, b, 1 - x), core), device((a, 1 - b, x), core),
                    device((flip, b, x), core), device(((a + 2) % NA, b, x), core)]
        self.buf = buf
        self.copies = [pltpu.make_async_remote_copy(
            src_ref=buf.at[2 * i], dst_ref=buf.at[2 * i + 1], send_sem=send.at[i], recv_sem=recv.at[i],
            device_id=p, device_id_type=MESH) for i, p in enumerate(partners)]
        self.n = len(partners)

    def start(self, i):
        self.copies[i].start()

    def end(self, i):
        self.copies[i].wait()
        self.buf[2 * i + 2] = self.buf[2 * i] + self.buf[2 * i + 1]

    def hooks(self, first, gap):
        table = {}
        for i in range(self.n):
            table.setdefault(first + i * gap, []).append(functools.partial(self.start, i))
            table.setdefault(first + i * gap + gap - 2, []).append(functools.partial(self.end, i))
        return table


def gather_kernel(parts, rows, mats, own_ref, count_ref, *refs):
    nm = len(mats)
    outs, vec_ref, total_ref = refs[:nm], refs[nm], refs[nm + 1]
    slots, flat_ref, send, recv, tbuf, tsend, trecv, osem = refs[nm + 2:nm + 10]
    mat_refs = refs[nm + 10:]
    pos, core = coords()
    me = flat(pos, core)
    slots[me, 0:rows, :] = own_ref[...].astype(BF16)
    if slots.shape[1] > rows:
        slots[me, rows:, :] = jnp.zeros((slots.shape[1] - rows, 128), BF16)
    tbuf[0] = count_ref[...]
    total = Total(pos, core, tbuf, tsend, trecv)
    greet(pos, core)
    hooks = total.hooks(6, 14)
    plan = steps()
    order_k = []
    for rel in plan:
        for col in range(3):
            order_k.append((rel, col))

    def chunk(idx, col):
        lo, n = parts[col]
        return slots.at[idx, pl.ds(lo, n), :]

    def copy(idx, col, k, direction, to):
        return pltpu.make_async_remote_copy(
            src_ref=chunk(idx, col), dst_ref=chunk(idx, col),
            send_sem=send.at[k, direction], recv_sem=recv.at[idx, col],
            device_id=to, device_id_type=MESH)

    def widen(idx):
        base = pl.multiple_of(idx * rows, 8)
        def body(i, _):
            r = pl.multiple_of(i * 112, 16)
            flat_ref[pl.ds(pl.multiple_of(base + r, 8), 112), :] = slots[idx, pl.ds(r, 112), :].astype(F32)
            return 0
        lax.fori_loop(0, rows // 112, body, 0)
        rest = rows % 112
        if rest:
            r = rows // 112 * 112
            flat_ref[pl.ds(pl.multiple_of(base + r, 8), rest), :] = slots[idx, r:r + rest, :].astype(F32)

    def run(k, rel, col, valid, src):
        def inner():
            idx = flat(src, core)
            if rel != (0, 0, 0):
                copy(idx, col, k, 0, device(pos, 1 - core)).wait_recv()
            for cond, child, direction in children(rel, ORDERS[col], pos):
                when(cond, lambda child=child, direction=direction: copy(idx, col, k, direction, device(child, core)).start())
            copy(idx, col, k, 4, device(pos, 1 - core)).start()
        when(valid, inner)

    def sibling(rel, k0):
        valid, src = source_of(rel, pos)
        def inner():
            other = flat(src, 1 - core)
            for col in range(3):
                copy(other, col, k0 + col, 4, device(pos, 1 - core)).wait_recv()
            widen(flat(src, core))
            widen(other)
        when(valid, inner)

    def finish(k, rel, col, valid, src):
        def inner():
            idx = flat(src, core)
            for cond, child, direction in children(rel, ORDERS[col], pos):
                when(cond, lambda child=child, direction=direction: copy(idx, col, k, direction, device(child, core)).wait_send())
            copy(idx, col, k, 4, device(pos, 1 - core)).wait_send()
        when(valid, inner)

    LAG = 2
    for i, rel in enumerate(plan):
        valid, src = source_of(rel, pos)
        for col in range(3):
            k = 3 * i + col
            run(k, rel, col, valid, src)
            for h in hooks.get(k, ()):
                h()
        if i >= LAG:
            sibling(plan[i - LAG], 3 * (i - LAG))
    for i in range(len(plan) - LAG, len(plan)):
        sibling(plan[i], 3 * i)
    total_ref[...] = tbuf[2 * total.n]
    first = 0
    copies = []
    for (height, width), mat, out, s in zip(mats, mat_refs, outs, range(nm)):
        n = width // 128
        def body(i, _, mat=mat, n=n, first=first):
            r = pl.multiple_of(i * 16, 16)
            for j in range(n):
                mat[pl.ds(r, 16), 128 * j:128 * (j + 1)] = flat_ref[pl.ds(first + r * n + j, 16, stride=n), :].astype(BF16)
            return 0
        lax.fori_loop(0, height // 16, body, 0)
        cp = pltpu.make_async_copy(mat, out, osem.at[s])
        cp.start()
        copies.append(cp)
        first += height * n
    vec_ref[...] = flat_ref[first:first + vec_ref.shape[0], :]
    for i, rel in enumerate(plan):
        valid, src = source_of(rel, pos)
        for col in range(3):
            finish(3 * i + col, rel, col, valid, src)
    for cp in copies:
        cp.wait()


def gather(own, count, mats, vec_rows):
    rows = own.shape[0]
    devices = 2 * NA * NB * NX
    slot = (rows + 15) // 16 * 16
    parts = split_rows(slot, SHARE)
    vm = pl.BlockSpec(memory_space=pltpu.VMEM)
    outs = [jax.ShapeDtypeStruct(m, BF16) for m in mats] + [
        jax.ShapeDtypeStruct((vec_rows, 128), F32), jax.ShapeDtypeStruct((8, 128), F32)]
    return pl.pallas_call(
        functools.partial(gather_kernel, parts, rows, mats),
        out_shape=outs,
        in_specs=[vm, vm],
        out_specs=[pl.BlockSpec(memory_space=pl.ANY)] * len(mats) + [vm, vm],
        scratch_shapes=[
            pltpu.VMEM((devices, slot, 128), BF16), pltpu.VMEM((devices * rows, 128), F32),
            pltpu.SemaphoreType.DMA((84, 5)), pltpu.SemaphoreType.DMA((devices, 3)),
            pltpu.VMEM((11, 8, 128), F32), pltpu.SemaphoreType.DMA((5,)), pltpu.SemaphoreType.DMA((5,)),
            pltpu.SemaphoreType.DMA((len(mats),))] + [pltpu.VMEM(m, BF16) for m in mats],
        compiler_params=pltpu.CompilerParams(collective_id=0, has_side_effects=True, vmem_limit_bytes=67043328),
        name="gather_params",
    )(own, count)


def reduce_kernel(parts, rows, grad_ref, part_ref, out_ref, total_ref, part, rb_core, rb_x, rb_b, rb_a01, rb_a2, stage, acc,
                  ssem, send_c, recv_c, send_p, recv_x, recv_b, recv_a, tbuf, tsend, trecv):
    pos, core = coords()
    plan = list(reversed(steps()))
    depth = stage.shape[0]
    loads = []
    for rel in plan:
        loads.append((rel, 1))
        loads.append((rel, 0))

    def load(i):
        rel, other = loads[i]
        valid, src = source_of(rel, pos)
        o = flat(src, 1 - core if other else core)
        return valid, o, pltpu.make_async_copy(grad_ref.at[pl.ds(pl.multiple_of(o * rows, 8), rows), :], stage.at[i % depth, 0:rows, :], ssem.at[i % depth])

    def start_load(i):
        valid, o, cp = load(i)
        when(valid, cp.start)

    tbuf[0] = part_ref[...]
    for i in range(depth):
        start_load(i)
    if stage.shape[1] > rows:
        for i in range(depth):
            stage[i, rows:, :] = jnp.zeros((stage.shape[1] - rows, 128), F32)
    total = Total(pos, core, tbuf, tsend, trecv)
    greet(pos, core)
    hooks = total.hooks(6, 14)

    def core_copy(rel):
        valid, src = source_of(rel, pos)
        chip = flat(src, 0) // 2
        return valid, src, pltpu.make_async_remote_copy(
            src_ref=part.at[flat(src, 1 - core)], dst_ref=rb_core.at[chip], send_sem=send_c.at[chip], recv_sem=recv_c.at[chip],
            device_id=device(pos, 1 - core), device_id_type=MESH)

    def convert(i):
        rel, other = loads[i]
        valid, o, cp = load(i)

        def inner():
            cp.wait()
            def body(t, _):
                r = pl.multiple_of(t * 16, 16)
                part[o, pl.ds(r, 16), :] = stage[i % depth, pl.ds(r, 16), :].astype(BF16)
                return 0
            lax.fori_loop(0, part.shape[1] // 16, body, 0, unroll=False)
        when(valid, inner)

    def buffer(direction, src, col):
        lo, n = parts[col]
        if direction == 3:
            return rb_x.at[src[0] * NB + src[1], pl.ds(lo, n), :], recv_x.at[src[0] * NB + src[1], col]
        if direction == 2:
            return rb_b.at[src[0] * NX + src[2], pl.ds(lo, n), :], recv_b.at[src[0] * NX + src[2], col]
        chip = (src[0] * NB + src[1]) * NX + src[2]
        if col == 2:
            return rb_a2.at[direction, chip], recv_a.at[direction, chip, col]
        return rb_a01.at[direction, src[0], pl.ds(lo, n), :], recv_a.at[direction, chip, col]

    def parent_copy(rel, col, k, src):
        order = ORDERS[col]
        d = [d for d in order if rel[d] != 0][-1]
        to = list(pos)
        if d == 0:
            direction = 0 if rel[0] < 0 else 1
            to[0] = pos[0] - 1 if rel[0] < 0 else pos[0] + 1
        else:
            direction = 1 + d
            to[d] = 1 - pos[d]
        lo, n = parts[col]
        dst, sem = buffer(direction, src, col)
        return pltpu.make_async_remote_copy(
            src_ref=part.at[flat(src, core), pl.ds(lo, n), :], dst_ref=dst, send_sem=send_p.at[k], recv_sem=sem,
            device_id=device(to, core), device_id_type=MESH)

    def arrived(direction, src, col):
        dst, sem = buffer(direction, src, col)
        return pltpu.make_async_remote_copy(src_ref=dst, dst_ref=dst, send_sem=send_p.at[0], recv_sem=sem,
                                            device_id=device(pos, 1 - core), device_id_type=MESH)

    def combine(k, rel, col):
        valid, src = source_of(rel, pos)
        lo, n = parts[col]

        def inner():
            o = flat(src, core)
            chip = flat(src, 0) // 2
            if col == 0:
                core_copy(rel)[2].wait_recv()
            kids = children(rel, ORDERS[col], pos)
            sure = [d for c, _, d in kids if c is None]
            maybe = [(c, d) for c, _, d in kids if c is not None]
            for d in sure:
                arrived(d, src, col).wait_recv()
            refs = [buffer(d, src, col)[0] for d in sure]

            def fold(write):
                def body(t, _):
                    r = pl.multiple_of(t * 16, 16)
                    v = part[o, pl.ds(lo + r, 16), :].astype(F32) + rb_core[chip, pl.ds(lo + r, 16), :].astype(F32)
                    for ref in refs:
                        v = v + ref[pl.ds(r, 16), :].astype(F32)
                    write(r, v)
                    return 0
                lax.fori_loop(0, n // 16, body, 0)

            root = rel == (0, 0, 0)

            def emit(r, v):
                if root:
                    out_ref[pl.ds(lo + r, 16), :] = v
                else:
                    part[o, pl.ds(lo + r, 16), :] = v.astype(BF16)

            def to_acc(r, v):
                acc[pl.ds(r, 16), :] = v

            if not maybe:
                fold(emit)
            else:
                fold(to_acc)
                for c, d in maybe:
                    def add(d=d):
                        arrived(d, src, col).wait_recv()
                        ref = buffer(d, src, col)[0]
                        def body(t, _):
                            r = pl.multiple_of(t * 16, 16)
                            acc[pl.ds(r, 16), :] = acc[pl.ds(r, 16), :] + ref[pl.ds(r, 16), :].astype(F32)
                            return 0
                        lax.fori_loop(0, n // 16, body, 0)
                    when(c, add)
                def last(t, _):
                    r = pl.multiple_of(t * 16, 16)
                    emit(r, acc[pl.ds(r, 16), :])
                    return 0
                lax.fori_loop(0, n // 16, last, 0)
            if not root:
                parent_copy(rel, col, k, src).start()
        when(valid, inner)

    AHEAD = 2
    def prepare(j):
        for i in (2 * j, 2 * j + 1):
            convert(i)
            if i + depth < len(loads):
                start_load(i + depth)
            if i % 2 == 0:
                valid, src, cp = core_copy(plan[j])
                when(valid, cp.start)
    for j in range(AHEAD):
        prepare(j)
    for j in range(len(plan)):
        if j + AHEAD < len(plan):
            prepare(j + AHEAD)
        for col in range(3):
            combine(3 * j + col, plan[j], col)
            for h in hooks.get(3 * j + col, ()):
                h()
    total_ref[...] = tbuf[2 * total.n]
    for j, rel in enumerate(plan):
        valid, src, cp = core_copy(rel)
        when(valid, cp.wait_send)
        if rel != (0, 0, 0):
            for col in range(3):
                when(valid, parent_copy(rel, col, 3 * j + col, src).wait_send)


def reduce(grad, part, rows):
    devices = 2 * NA * NB * NX
    slot = (rows + 15) // 16 * 16
    parts = split_rows(slot, SHARE)
    two = parts[0][1] + parts[1][1]
    vm = pl.BlockSpec(memory_space=pltpu.VMEM)
    return pl.pallas_call(
        functools.partial(reduce_kernel, parts, rows),
        out_shape=[jax.ShapeDtypeStruct((slot, 128), F32), jax.ShapeDtypeStruct((8, 128), F32)],
        in_specs=[pl.BlockSpec(memory_space=pl.ANY), vm],
        out_specs=[vm, vm],
        scratch_shapes=[
            pltpu.VMEM((devices, slot, 128), BF16), pltpu.VMEM((devices // 2, slot, 128), BF16),
            pltpu.VMEM((NA * NB, slot, 128), BF16), pltpu.VMEM((NA * NX, slot, 128), BF16),
            pltpu.VMEM((2, NA, two, 128), BF16), pltpu.VMEM((2, devices // 2, parts[2][1], 128), BF16),
            pltpu.VMEM((4, slot, 128), F32), pltpu.VMEM((max(p[1] for p in parts), 128), F32),
            pltpu.SemaphoreType.DMA((4,)), pltpu.SemaphoreType.DMA((devices // 2,)), pltpu.SemaphoreType.DMA((devices // 2,)),
            pltpu.SemaphoreType.DMA((84,)), pltpu.SemaphoreType.DMA((NA * NB, 3)), pltpu.SemaphoreType.DMA((NA * NX, 3)),
            pltpu.SemaphoreType.DMA((2, devices // 2, 3)),
            pltpu.VMEM((11, 8, 128), F32), pltpu.SemaphoreType.DMA((5,)), pltpu.SemaphoreType.DMA((5,))],
        compiler_params=pltpu.CompilerParams(collective_id=1, has_side_effects=True, vmem_limit_bytes=67043328),
        name="reduce_gradient",
    )(grad, part)


ERF_TOP = (0.00022905065861350646, 0.0034082910107109506, 0.050955695062380861, 0.18520832239976145, 1.128379143519084)
ERF_LOW = (-1.1791602954361697e-7, 0.000023547966471313185, 0.0010179625278914885, 0.014070470171167667,
           0.11098505178285362, 0.49746925110067538, 1.0)


def erf(v):
    v = jnp.clip(v, -3.832506856900711, 3.832506856900711)
    s = v * v
    top = ERF_TOP[0]
    for c in ERF_TOP[1:]:
        top = top * s + c
    low = ERF_LOW[0]
    for c in ERF_LOW[1:]:
        low = low * s + c
    return v * top / low


def dot(a, b):
    return jnp.dot(a, b, preferred_element_type=F32)


def dot_nt(a, b):
    return lax.dot_general(a, b, (((1,), (1,)), ((), ())), preferred_element_type=F32)


def dot_tn(a, b):
    return lax.dot_general(a, b, (((0,), (0,)), ((), ())), preferred_element_type=F32)


def loop(n, body):
    def step(i, carry):
        body(i)
        return carry
    lax.fori_loop(0, n, step, 0)


def at(i, size):
    return pl.ds(pl.multiple_of(i * size, size), size)


def compute_kernel(rows_total, x_ref, target_ref, mask_ref, vec_ref, count_ref, wq_hbm, wp_hbm, wi_hbm, wo_hbm,
                   act_ref, igrad_ref, sq_ref, grad_hbm,
                   wq, wp, wi, wo, mixed, probs, att, middle, slope, active, left, gout, glow, ghid, gmix, stage, vstage, wsem, ssem):
    tokens = x_ref.shape[0]
    scale = HEAD ** (-0.5)
    loads = [pltpu.make_async_copy(h, w, wsem.at[i]) for i, (h, w) in enumerate(
        ((wq_hbm, wq), (wp_hbm, wp), (wi_hbm, wi), (wo_hbm, wo)))]
    for c in loads:
        c.start()
    used_rows = (3 * D * D + D * D + 2 * D * FF) // 128

    def vector(row, n):
        return jnp.concatenate([vec_ref[row + j:row + j + 1, :] for j in range(n)], axis=1)

    per = D // 128
    gain_one, shift_one, bias_query, bias_value, bias_proj, gain_two, shift_two, bias_out = [
        vector(per * i, per) for i in range(8)]
    bias_in_row = 8 * per
    vstage[...] = jnp.zeros_like(vstage)

    def put_vector(i, v):
        for j in range(v.shape[1] // 128):
            vstage[per * i + j:per * i + j + 1, :] = v[:, 128 * j:128 * (j + 1)]

    def stats(v):
        mean = jnp.mean(v, -1, keepdims=True)
        center = v - mean
        r = lax.rsqrt(jnp.mean(center * center, -1, keepdims=True) + norm_epsilon)
        return center * r, r

    RB = 128
    nrb = tokens // RB
    low = glow

    def flip(dst):
        def body(i):
            left[dst, at(i, 128), :] = low[:, at(i, 128)].T
        loop(D // 128, body)

    def ln_one(i):
        z, _ = stats(x_ref[at(i, RB), :].astype(F32))
        low[at(i, RB), :] = (z * gain_one + shift_one).astype(BF16)
    loop(nrb, ln_one)
    loads[0].wait()
    BN = 256

    def qkv(part, bias):
        def body(i):
            j = i + part * (D // BN)
            v = dot(low[...], wq[:, at(j, BN)])
            if bias is not None:
                v = v + vec_bias[0:1, at(i, BN)]
            mixed[:, at(j, BN)] = v.astype(BF16)
        loop(D // BN, body)
    vec_bias = middle
    middle[0:1, :] = bias_query
    qkv(0, True)
    qkv(1, None)
    middle[0:1, :] = bias_value
    qkv(2, True)
    flip(0)

    pairs = HEADS // 2
    lane = lax.broadcasted_iota(jnp.int32, (128, 128), 1)
    lower = lane < HEAD
    r256 = lax.broadcasted_iota(jnp.int32, (128, 256), 0) // FRAMES
    c256 = (lax.broadcasted_iota(jnp.int32, (128, 256), 1) % 128) // FRAMES
    same = r256 == c256

    def stack(v):
        zero = jnp.zeros_like(v)
        return jnp.concatenate([jnp.where(lower, v, zero), jnp.where(lower, zero, v)], axis=0)

    def tile(i):
        g, p = i // pairs, i % pairs
        rows = at(g, 128)
        return rows, p

    def attention(i):
        rows, p = tile(i)
        q = mixed[rows, at(p, 128)]
        k = mixed[rows, at(p + pairs, 128)]
        v = mixed[rows, at(p + 2 * pairs, 128)]
        s = dot_nt(q, stack(k)) * scale
        s = jnp.where(same, s, -1e30)
        out = []
        for h in range(2):
            sh = s[:, 128 * h:128 * (h + 1)]
            e = jnp.exp(sh - jnp.max(sh, -1, keepdims=True))
            out.append(e / jnp.sum(e, -1, keepdims=True))
        pr = jnp.concatenate(out, axis=1)
        probs[i] = pr
        att[rows, at(p, 128)] = dot(pr.astype(BF16), stack(v)).astype(BF16)
    loop(pairs * (tokens // 128), attention)

    loads[1].wait()

    def project(i):
        v = dot(att[at(i, RB), :], wp[...])
        m = x_ref[at(i, RB), :].astype(F32) + (v + bias_proj)
        middle[at(i, RB), :] = m
        z, _ = stats(m)
        low[at(i, RB), :] = (z * gain_two + shift_two).astype(BF16)
    loop(nrb, project)
    loads[2].wait()

    def hidden(i):
        bias = jnp.concatenate([vec_ref[pl.ds(bias_in_row + 2 * i + j, 1), :] for j in range(BN // 128)], axis=1)
        h = dot(low[...], wi[:, at(i, BN)]) + bias
        cdf = 0.5 * (1.0 + erf(h * (0.5 ** 0.5)))
        pdf = jnp.exp(-0.5 * h * h) * (1.0 / math.sqrt(2.0 * math.pi))
        active[:, at(i, BN)] = (h * cdf).astype(BF16)
        slope[:, at(i, BN)] = cdf + h * pdf
    loop(FF // BN, hidden)
    flip(2)
    loads[3].wait()

    def second(i):
        gout[:, at(i, BN)] = dot_nt(active[...], wo[at(i, BN), :])
    loop(D // BN, second)
    factor = 2.0 / (count_ref[0:1, 0:1] * D)
    sq_ref[...] = jnp.zeros_like(sq_ref)

    def finish(i):
        o = middle[at(i, RB), :] + (gout[at(i, RB), :] + bias_out)
        act_ref[at(i, RB), :] = o.astype(BF16)
        misfit = o - target_ref[at(i, RB), :].astype(F32)
        m = mask_ref[at(i, RB), :]
        sq_ref[...] += jnp.full(sq_ref.shape, jnp.sum(m * jnp.sum(misfit * misfit, -1, keepdims=True)))
        g = (factor * m) * misfit
        gout[at(i, RB), :] = g
        low[at(i, RB), :] = g.astype(BF16)
    loop(nrb, finish)
    flip(3)

    def colsum(ref):
        return jnp.sum(ref.astype(F32), 0, keepdims=True)

    put_vector(7, colsum(low[...]))

    sent = []

    def weight_grad(lhs, rhs, width, first):
        n = width // 128
        half = D // 2
        for h in range(2):
            slot = len(sent) % 2
            if len(sent) >= 2:
                sent[-2].wait()
            size = half * n

            def body(j):
                v = dot(left[lhs, h * half:(h + 1) * half, :], rhs[:, at(j, BN)])
                for t in range(BN // 128):
                    stage[slot, pl.ds(2 * j + t, half, stride=n), :] = v[:, 128 * t:128 * (t + 1)]
            loop(width // BN, body)
            cp = pltpu.make_async_copy(stage.at[slot, 0:size, :], grad_hbm.at[first + h * size:first + (h + 1) * size, :], ssem.at[slot])
            cp.start()
            sent.append(cp)

    row_proj = 3 * D * D // 128
    row_in = row_proj + D * D // 128
    row_out = row_in + D * FF // 128
    weight_grad(3, active, FF, row_out)

    def back_hidden(i):
        v = dot(low[...], wo[:, at(i, BN)]) * slope[:, at(i, BN)]
        b = v.astype(BF16)
        ghid[:, at(i, BN)] = b
        s = jnp.sum(b.astype(F32), 0, keepdims=True)
        for t in range(BN // 128):
            vstage[pl.ds(bias_in_row + 2 * i + t, 1), :] = s[:, 128 * t:128 * (t + 1)]
    loop(FF // BN, back_hidden)
    weight_grad(2, ghid, FF, row_in)

    dnorm = igrad_ref

    def back_in(i):
        dnorm[:, at(i, BN)] = dot_nt(ghid[...], wi[at(i, BN), :])
    loop(D // BN, back_in)

    def norm_back(values, gain, dy):
        z, r = stats(values)
        dz = dy * gain
        m1 = jnp.mean(dz, -1, keepdims=True)
        m2 = jnp.mean(dz * z, -1, keepdims=True)
        return r * (dz - m1 - z * m2), jnp.sum(dy * z, 0, keepdims=True), jnp.sum(dy, 0, keepdims=True)

    zero = jnp.zeros((1, D), F32)

    def ln_two_back(i, carry):
        a, b, c = carry
        d, dg, ds = norm_back(middle[at(i, RB), :], gain_two, dnorm[at(i, RB), :])
        g = gout[at(i, RB), :] + d
        gout[at(i, RB), :] = g
        gl = g.astype(BF16)
        low[at(i, RB), :] = gl
        return a + dg, b + ds, c + jnp.sum(gl.astype(F32), 0, keepdims=True)
    a, b, c = lax.fori_loop(0, nrb, ln_two_back, (zero, zero, zero))
    put_vector(5, a)
    put_vector(6, b)
    put_vector(4, c)

    def flip_att(i):
        left[1, at(i, 128), :] = att[:, at(i, 128)].T
    loop(D // 128, flip_att)
    weight_grad(1, low, D, row_proj)

    def back_proj(i):
        att[:, at(i, BN)] = dot_nt(low[...], wp[at(i, BN), :]).astype(BF16)
    loop(D // BN, back_proj)

    def attention_back(i):
        rows, p = tile(i)
        q = mixed[rows, at(p, 128)]
        k = mixed[rows, at(p + pairs, 128)]
        v = mixed[rows, at(p + 2 * pairs, 128)]
        do = att[rows, at(p, 128)]
        pr = probs[i]
        dp = dot_nt(do, stack(v))
        out = []
        for h in range(2):
            ph, dh = pr[:, 128 * h:128 * (h + 1)], dp[:, 128 * h:128 * (h + 1)]
            out.append((ph * (dh - jnp.sum(ph * dh, -1, keepdims=True))).astype(BF16))
        gmix[rows, at(p, 128)] = (dot(jnp.concatenate(out, axis=1), stack(k)) * scale).astype(BF16)
        gmix[rows, at(p + pairs, 128)] = (dot_tn(jnp.concatenate(out, axis=0), stack(q)) * scale).astype(BF16)
        pl_low = jnp.concatenate([pr[:, :128], pr[:, 128:]], axis=0).astype(BF16)
        gmix[rows, at(p + 2 * pairs, 128)] = dot_tn(pl_low, stack(do)).astype(BF16)
    loop(pairs * (tokens // 128), attention_back)
    put_vector(2, colsum(gmix[:, 0:D]))
    put_vector(3, colsum(gmix[:, 2 * D:3 * D]))
    weight_grad(0, gmix, 3 * D, 0)

    def back_qkv(i):
        dnorm[:, at(i, BN)] = dot_nt(gmix[...], wq[at(i, BN), :])
    loop(D // BN, back_qkv)
    whole = rows_total

    def ln_one_back(i, carry):
        a, b = carry
        d, dg, ds = norm_back(x_ref[at(i, RB), :].astype(F32), gain_one, dnorm[at(i, RB), :])
        igrad_ref[at(i, RB), :] = (gout[at(i, RB), :] + d) * whole
        return a + dg, b + ds
    a, b = lax.fori_loop(0, nrb, ln_one_back, (zero, zero))
    put_vector(0, a)
    put_vector(1, b)
    sent[-2].wait()
    sent[-1].wait()
    cp = pltpu.make_async_copy(vstage, grad_hbm.at[used_rows:used_rows + vstage.shape[0], :], ssem.at[0])
    cp.start()
    cp.wait()


def compute(tokens, target, mask, vectors, count, weights, whole, total_rows):
    n = tokens.shape[0]
    vm = pl.BlockSpec(memory_space=pltpu.VMEM)
    anyspace = pl.BlockSpec(memory_space=pl.ANY)
    used_rows = (3 * D * D + D * D + 2 * D * FF) // 128
    return pl.pallas_call(
        functools.partial(compute_kernel, float(whole)),
        out_shape=[jax.ShapeDtypeStruct((n, D), BF16), jax.ShapeDtypeStruct((n, D), F32),
                   jax.ShapeDtypeStruct((8, 128), F32), jax.ShapeDtypeStruct((total_rows, 128), F32)],
        in_specs=[vm] * 5 + [anyspace] * 4,
        out_specs=[vm, vm, vm, anyspace],
        scratch_shapes=[
            pltpu.VMEM((D, 3 * D), BF16), pltpu.VMEM((D, D), BF16), pltpu.VMEM((D, FF), BF16), pltpu.VMEM((D, FF), BF16),
            pltpu.VMEM((n, 3 * D), BF16), pltpu.VMEM((HEADS // 2 * (n // 128), 128, 256), F32), pltpu.VMEM((n, D), BF16),
            pltpu.VMEM((n, D), F32), pltpu.VMEM((n, FF), F32), pltpu.VMEM((n, FF), BF16), pltpu.VMEM((4, D, n), BF16),
            pltpu.VMEM((n, D), F32), pltpu.VMEM((n, D), BF16), pltpu.VMEM((n, FF), BF16), pltpu.VMEM((n, 3 * D), BF16),
            pltpu.VMEM((2, D // 2 * FF // 128, 128), F32), pltpu.VMEM((total_rows - used_rows, 128), F32),
            pltpu.SemaphoreType.DMA((4,)), pltpu.SemaphoreType.DMA((2,))],
        compiler_params=pltpu.CompilerParams(vmem_limit_bytes=67043328),
        name="layer",
    )(tokens, target, mask, vectors, count, *weights)


MATS = ((D, 3 * D), (D, D), (D, FF), (D, FF))


def shards(custom, tokens, valid_mask, target, params, first_moment, second_moment):
    devices = lax.axis_size("dp") * lax.axis_size("fsdp")
    total_rows = params.shape[0] * devices
    used_rows = sum(h * w for h, w in MATS) // 128
    mask_values = valid_mask.astype(jnp.float32)
    count = jnp.full((8, 128), jnp.sum(mask_values))
    if custom:
        *weights, vectors, count = gather(params, count, MATS, total_rows - used_rows)
    else:
        whole = collect(params)
        weights = unpack(whole)[:4]
        vectors = whole[used_rows:].astype(jnp.float32)
        count = lax.psum(count, ("dp", "fsdp"))
    activations, input_grad, squares, grad = compute(
        tokens, target, mask_values.reshape(-1, 1), vectors, count, weights, tokens.shape[0] * devices * D, total_rows
    )
    if custom:
        gradient, squares = reduce(grad, squares, params.shape[0])
        gradient = gradient[: params.shape[0]]
    else:
        gradient = reduce_rows(grad)
        squares = lax.psum(squares, ("dp", "fsdp"))
    loss = squares[0, 0] / (count[0, 0] * D)
    new_first = beta_one * first_moment + (1.0 - beta_one) * gradient
    new_second = beta_two * second_moment + (1.0 - beta_two) * gradient * gradient
    first_hat = new_first / (1.0 - beta_one**STEP)
    second_hat = new_second / (1.0 - beta_two**STEP)
    new_params = params - learn_rate * (
        first_hat / (jnp.sqrt(second_hat) + adam_epsilon) + weight_decay * params
    )
    return (activations, loss, input_grad, new_params, new_first, new_second)


def solution(mesh):
    rows = P(("dp", "fsdp"), None)
    custom = mesh.shape["dp"] == NA * NB and mesh.shape["fsdp"] == 2 * NX
    return jax.shard_map(
        functools.partial(shards, custom),
        mesh=mesh,
        in_specs=(rows, P(("dp", "fsdp")), rows, rows, rows, rows),
        out_specs=(rows, P(), rows, rows, rows, rows),
        check_vma=False,
    )
```

profile of v0, /device:TPU:0, one launch (start us, length us, event | category | flops | bytes accessed | tf_op | source)
XLA Modules:
  0.0 253.9 jit_solution(12095800786482168533)
XLA Ops:
  0.6 1.3 convert_reduce_fusion
  1.9 1.2 broadcast_in_dim.3.count_ref
  3.2 76.5 %gather_params.1 = (bf16[768,2304]{1,0:T(8,128)(2,1)}, bf16[768,768]{1,0:T(8,128)(2,1)}, bf16[768,3072]{1,0:T(8,128)(2,1)}, bf16[768,3072]{1,0:T(8,128)(2,1)}, f32[256,128]{1,0:T(8,128)}, /*index=5*/f32[8,128]{1,0:T(8,128)}) custom-call(f32[1736,128]{1,0:T(8,128)} %own_ref.1, f32[8,128]{1,0:T(8,128)} %broadcast_in_dim.3.count_ref), custom_call_target="tpu_custom_call" | custom-call | tf_op jit(solution)/shard_map/gather_params/pallas_call | solution.py:299
  79.7 0.7 convert_element_type.3
  80.3 0.9 copy.12.mask_ref
  81.2 85.8 %layer.1 = (bf16[512,768]{1,0:T(8,128)(2,1)}, f32[512,768]{1,0:T(8,128)}, f32[8,128]{1,0:T(8,128)}, f32[55552,128]{1,0:T(8,128)}) custom-call(bf16[512,768]{1,0:T(8,128)(2,1)} %x_ref.1, bf16[512,768]{1,0:T(8,128)(2,1)} %target_ref.1, f32[512,1]{1,0:T(8,128)} %copy.12.mask_ref, f32[256,128]{1,0:T(8,128)} %get-tuple-element.18.vec_ref, ...), custom_call_target="tpu_custom_call" | custom-call | tf_op jit(solution)/shard_map/layer/pallas_call | solution.py:806
  167.1 78.1 %reduce_gradient.1 = (f32[1744,128]{1,0:T(8,128)}, f32[8,128]{1,0:T(8,128)}) custom-call(f32[55552,128]{1,0:T(8,128)} %get-tuple-element.25.grad_ref, f32[8,128]{1,0:T(8,128)} %get-tuple-element.26.part_ref), custom_call_target="tpu_custom_call" | custom-call | tf_op jit(solution)/shard_map/reduce_gradient/pallas_call | solution.py:489
  245.2 3.9 %multiply_subtract_fusion = (f32[1736,128]{1,0:T(8,128)}, f32[1736,128]{1,0:T(8,128)}, f32[1736,128]{1,0:T(8,128)}) fusion(f32[1736,128]{1,0:T(8,128)} %own_ref.1, f32[1744,128]{1,0:T(8,128)} %get-tuple-element.29, f32[1736,128]{1,0:T(8,128)} %param.10, f32[1736,128]{1,0:T(8,128)} %param.11), kind=kLoop, calls=%fused_computation.2 | loop fusion | flops 3333120 | bytes 6221824 | tf_op jit(solution)/shard_map/sub | solution.py:854
  249.0 1.2 slice.9
  250.2 1.2 slice.10
where the time goes:
time: 254 us
  Pallas kernels  240 us (94%)
  other arithmetic  5.86 us (2%)
  local copies, waits for them, and re-layouts  4.49 us (2%)
  between operations  3.08 us (1%)
    pallas_call x1, Pallas kernels, compute(): pl.pallas_call(functools.partial(compute_kernel, float(whole)), out_shape...  85.8 us
    pallas_call x1, Pallas kernels, reduce(): pl.pallas_call(functools.partial(reduce_kernel, parts, rows), out_shape=[...  78.1 us
    pallas_call x1, Pallas kernels, gather(): pl.pallas_call(functools.partial(gather_kernel, parts, rows, mats), out_s...  76.5 us

commit v1 on v0

--- a/solution.py
+++ b/solution.py
@@ -182,7 +182,7 @@
         return table
 
 
-def gather_kernel(parts, rows, mats, own_ref, count_ref, *refs):
+def gather_kernel(parts, rows, mats, own_ref, mask_ref, *refs):
     nm = len(mats)
     outs, vec_ref, total_ref = refs[:nm], refs[nm], refs[nm + 1]
     slots, flat_ref, send, recv, tbuf, tsend, trecv, osem = refs[nm + 2:nm + 10]
@@ -192,7 +192,7 @@
     slots[me, 0:rows, :] = own_ref[...].astype(BF16)
     if slots.shape[1] > rows:
         slots[me, rows:, :] = jnp.zeros((slots.shape[1] - rows, 128), BF16)
-    tbuf[0] = count_ref[...]
+    tbuf[0] = jnp.full(tbuf.shape[1:], jnp.sum(mask_ref[...].astype(F32)))
     total = Total(pos, core, tbuf, tsend, trecv)
     greet(pos, core)
     hooks = total.hooks(6, 14)
@@ -288,7 +288,7 @@
         cp.wait()
 
 
-def gather(own, count, mats, vec_rows):
+def gather(own, mask, mats, vec_rows):
     rows = own.shape[0]
     devices = 2 * NA * NB * NX
     slot = (rows + 15) // 16 * 16
@@ -308,10 +308,20 @@
             pltpu.SemaphoreType.DMA((len(mats),))] + [pltpu.VMEM(m, BF16) for m in mats],
         compiler_params=pltpu.CompilerParams(collective_id=0, has_side_effects=True, vmem_limit_bytes=67043328),
         name="gather_params",
-    )(own, count)
-
-
-def reduce_kernel(parts, rows, grad_ref, part_ref, out_ref, total_ref, part, rb_core, rb_x, rb_b, rb_a01, rb_a2, stage, acc,
+    )(own, mask)
+
+
+def sweep(n, body, block=112):
+    if n // block:
+        def step(i, carry):
+            body(pl.multiple_of(i * block, 16), block)
+            return carry
+        lax.fori_loop(0, n // block, step, 0)
+    if n % block:
+        body(n // block * block, n % block)
+
+
+def reduce_kernel(parts, rows, grad_ref, part_ref, count_ref, out_ref, loss_ref, part, rb_core, rb_x, rb_b, rb_a01, rb_a2, stage, acc,
                   ssem, send_c, recv_c, send_p, recv_x, recv_b, recv_a, tbuf, tsend, trecv):
     pos, core = coords()
     plan = list(reversed(steps()))
@@ -354,11 +364,9 @@
 
         def inner():
             cp.wait()
-            def body(t, _):
-                r = pl.multiple_of(t * 16, 16)
-                part[o, pl.ds(r, 16), :] = stage[i % depth, pl.ds(r, 16), :].astype(BF16)
-                return 0
-            lax.fori_loop(0, part.shape[1] // 16, body, 0, unroll=False)
+            def body(r, m):
+                part[o, pl.ds(r, m), :] = stage[i % depth, pl.ds(r, m), :].astype(BF16)
+            sweep(part.shape[1], body)
         when(valid, inner)
 
     def buffer(direction, src, col):
@@ -410,25 +418,23 @@
             refs = [buffer(d, src, col)[0] for d in sure]
 
             def fold(write):
-                def body(t, _):
-                    r = pl.multiple_of(t * 16, 16)
-                    v = part[o, pl.ds(lo + r, 16), :].astype(F32) + rb_core[chip, pl.ds(lo + r, 16), :].astype(F32)
+                def body(r, m):
+                    v = part[o, pl.ds(lo + r, m), :].astype(F32) + rb_core[chip, pl.ds(lo + r, m), :].astype(F32)
                     for ref in refs:
-                        v = v + ref[pl.ds(r, 16), :].astype(F32)
-                    write(r, v)
-                    return 0
-                lax.fori_loop(0, n // 16, body, 0)
+                        v = v + ref[pl.ds(r, m), :].astype(F32)
+                    write(r, m, v)
+                sweep(n, body)
 
             root = rel == (0, 0, 0)
 
-            def emit(r, v):
+            def emit(r, m, v):
                 if root:
-                    out_ref[pl.ds(lo + r, 16), :] = v
+                    out_ref[pl.ds(lo + r, m), :] = v
                 else:
-                    part[o, pl.ds(lo + r, 16), :] = v.astype(BF16)
-
-            def to_acc(r, v):
-                acc[pl.ds(r, 16), :] = v
+                    part[o, pl.ds(lo + r, m), :] = v.astype(BF16)
+
+            def to_acc(r, m, v):
+                acc[pl.ds(r, m), :] = v
 
             if not maybe:
                 fold(emit)
@@ -438,22 +444,18 @@
                     def add(d=d):
                         arrived(d, src, col).wait_recv()
                         ref = buffer(d, src, col)[0]
-                        def body(t, _):
-                            r = pl.multiple_of(t * 16, 16)
-                            acc[pl.ds(r, 16), :] = acc[pl.ds(r, 16), :] + ref[pl.ds(r, 16), :].astype(F32)
-                            return 0
-                        lax.fori_loop(0, n // 16, body, 0)
+                        def body(r, m):
+                            acc[pl.ds(r, m), :] = acc[pl.ds(r, m), :] + ref[pl.ds(r, m), :].astype(F32)
+                        sweep(n, body)
                     when(c, add)
-                def last(t, _):
-                    r = pl.multiple_of(t * 16, 16)
-                    emit(r, acc[pl.ds(r, 16), :])
-                    return 0
-                lax.fori_loop(0, n // 16, last, 0)
+                def last(r, m):
+                    emit(r, m, acc[pl.ds(r, m), :])
+                sweep(n, last)
             if not root:
                 parent_copy(rel, col, k, src).start()
         when(valid, inner)
 
-    AHEAD = 2
+    AHEAD = 4
     def prepare(j):
         for i in (2 * j, 2 * j + 1):
             convert(i)
@@ -471,7 +473,8 @@
             combine(3 * j + col, plan[j], col)
             for h in hooks.get(3 * j + col, ()):
                 h()
-    total_ref[...] = tbuf[2 * total.n]
+    quotient = tbuf[2 * total.n] / (count_ref[...] * D)
+    loss_ref[0, 0] = quotient[0, 0]
     for j, rel in enumerate(plan):
         valid, src, cp = core_copy(rel)
         when(valid, cp.wait_send)
@@ -480,7 +483,7 @@
                 when(valid, parent_copy(rel, col, 3 * j + col, src).wait_send)
 
 
-def reduce(grad, part, rows):
+def reduce(grad, part, count, rows):
     devices = 2 * NA * NB * NX
     slot = (rows + 15) // 16 * 16
     parts = split_rows(slot, SHARE)
@@ -488,9 +491,9 @@
     vm = pl.BlockSpec(memory_space=pltpu.VMEM)
     return pl.pallas_call(
         functools.partial(reduce_kernel, parts, rows),
-        out_shape=[jax.ShapeDtypeStruct((slot, 128), F32), jax.ShapeDtypeStruct((8, 128), F32)],
-        in_specs=[pl.BlockSpec(memory_space=pl.ANY), vm],
-        out_specs=[vm, vm],
+        out_shape=[jax.ShapeDtypeStruct((slot, 128), F32), jax.ShapeDtypeStruct((1, 1), F32)],
+        in_specs=[pl.BlockSpec(memory_space=pl.ANY), vm, vm],
+        out_specs=[vm, pl.BlockSpec(memory_space=pltpu.SMEM)],
         scratch_shapes=[
             pltpu.VMEM((devices, slot, 128), BF16), pltpu.VMEM((devices // 2, slot, 128), BF16),
             pltpu.VMEM((NA * NB, slot, 128), BF16), pltpu.VMEM((NA * NX, slot, 128), BF16),
@@ -502,25 +505,10 @@
             pltpu.VMEM((11, 8, 128), F32), pltpu.SemaphoreType.DMA((5,)), pltpu.SemaphoreType.DMA((5,))],
         compiler_params=pltpu.CompilerParams(collective_id=1, has_side_effects=True, vmem_limit_bytes=67043328),
         name="reduce_gradient",
-    )(grad, part)
-
-
-ERF_TOP = (0.00022905065861350646, 0.0034082910107109506, 0.050955695062380861, 0.18520832239976145, 1.128379143519084)
-ERF_LOW = (-1.1791602954361697e-7, 0.000023547966471313185, 0.0010179625278914885, 0.014070470171167667,
-           0.11098505178285362, 0.49746925110067538, 1.0)
-
-
-def erf(v):
-    v = jnp.clip(v, -3.832506856900711, 3.832506856900711)
-    s = v * v
-    top = ERF_TOP[0]
-    for c in ERF_TOP[1:]:
-        top = top * s + c
-    low = ERF_LOW[0]
-    for c in ERF_LOW[1:]:
-        low = low * s + c
-    return v * top / low
-
+    )(grad, part, count)
+
+
+TILES = 12
 
 def dot(a, b):
     return jnp.dot(a, b, preferred_element_type=F32)
@@ -541,8 +529,15 @@
     lax.fori_loop(0, n, step, 0)
 
 
+def several(n, body):
+    def group(i):
+        for j in range(TILES):
+            body(i * TILES + j)
+    loop(n // TILES, group)
+
+
 def at(i, size):
-    return pl.ds(pl.multiple_of(i * size, size), size)
+    return pl.ds(i * size if isinstance(i, int) else pl.multiple_of(i * size, size), size)
 
 
 def compute_kernel(rows_total, x_ref, target_ref, mask_ref, vec_ref, count_ref, wq_hbm, wp_hbm, wi_hbm, wo_hbm,
@@ -552,8 +547,7 @@
     scale = HEAD ** (-0.5)
     loads = [pltpu.make_async_copy(h, w, wsem.at[i]) for i, (h, w) in enumerate(
         ((wq_hbm, wq), (wp_hbm, wp), (wi_hbm, wi), (wo_hbm, wo)))]
-    for c in loads:
-        c.start()
+    loads[0].start()
     used_rows = (3 * D * D + D * D + 2 * D * FF) // 128
 
     def vector(row, n):
@@ -575,7 +569,7 @@
         r = lax.rsqrt(jnp.mean(center * center, -1, keepdims=True) + norm_epsilon)
         return center * r, r
 
-    RB = 128
+    RB = 256
     nrb = tokens // RB
     low = glow
 
@@ -589,16 +583,24 @@
         low[at(i, RB), :] = (z * gain_one + shift_one).astype(BF16)
     loop(nrb, ln_one)
     loads[0].wait()
+    for c in loads[1:]:
+        c.start()
     BN = 256
+    WN = 768
+    HN = 768
+    GN = 768
+    SN = 256
+    QN = 768
+    IN = 256
 
     def qkv(part, bias):
         def body(i):
-            j = i + part * (D // BN)
-            v = dot(low[...], wq[:, at(j, BN)])
+            j = i + part * (D // QN)
+            v = dot(low[...], wq[:, at(j, QN)])
             if bias is not None:
-                v = v + vec_bias[0:1, at(i, BN)]
-            mixed[:, at(j, BN)] = v.astype(BF16)
-        loop(D // BN, body)
+                v = v + vec_bias[0:1, at(i, QN)]
+            mixed[:, at(j, QN)] = v.astype(BF16)
+        loop(D // QN, body)
     vec_bias = middle
     middle[0:1, :] = bias_query
     qkv(0, True)
@@ -638,7 +640,7 @@
         pr = jnp.concatenate(out, axis=1)
         probs[i] = pr
         att[rows, at(p, 128)] = dot(pr.astype(BF16), stack(v)).astype(BF16)
-    loop(pairs * (tokens // 128), attention)
+    several(pairs * (tokens // 128), attention)
 
     loads[1].wait()
 
@@ -652,32 +654,35 @@
     loads[2].wait()
 
     def hidden(i):
-        bias = jnp.concatenate([vec_ref[pl.ds(bias_in_row + 2 * i + j, 1), :] for j in range(BN // 128)], axis=1)
-        h = dot(low[...], wi[:, at(i, BN)]) + bias
-        cdf = 0.5 * (1.0 + erf(h * (0.5 ** 0.5)))
+        bias = jnp.concatenate([vec_ref[pl.ds(bias_in_row + HN // 128 * i + j, 1), :] for j in range(HN // 128)], axis=1)
+        h = dot(low[...], wi[:, at(i, HN)]) + bias
+        cdf = 0.5 * (1.0 + lax.erf(h * (0.5 ** 0.5)))
         pdf = jnp.exp(-0.5 * h * h) * (1.0 / math.sqrt(2.0 * math.pi))
-        active[:, at(i, BN)] = (h * cdf).astype(BF16)
-        slope[:, at(i, BN)] = cdf + h * pdf
-    loop(FF // BN, hidden)
+        active[:, at(i, HN)] = (h * cdf).astype(BF16)
+        slope[:, at(i, HN)] = cdf + h * pdf
+    loop(FF // HN, hidden)
     flip(2)
     loads[3].wait()
 
     def second(i):
-        gout[:, at(i, BN)] = dot_nt(active[...], wo[at(i, BN), :])
-    loop(D // BN, second)
+        gout[:, at(i, SN)] = dot_nt(active[...], wo[at(i, SN), :])
+    loop(D // SN, second)
     factor = 2.0 / (count_ref[0:1, 0:1] * D)
     sq_ref[...] = jnp.zeros_like(sq_ref)
+
+    mask_columns = mask_ref[...].astype(F32).T
 
     def finish(i):
         o = middle[at(i, RB), :] + (gout[at(i, RB), :] + bias_out)
         act_ref[at(i, RB), :] = o.astype(BF16)
         misfit = o - target_ref[at(i, RB), :].astype(F32)
-        m = mask_ref[at(i, RB), :]
+        m = jnp.concatenate([mask_columns[:, RB // 128 * i + j:RB // 128 * i + j + 1] for j in range(RB // 128)], axis=0)
         sq_ref[...] += jnp.full(sq_ref.shape, jnp.sum(m * jnp.sum(misfit * misfit, -1, keepdims=True)))
         g = (factor * m) * misfit
         gout[at(i, RB), :] = g
         low[at(i, RB), :] = g.astype(BF16)
-    loop(nrb, finish)
+    for i in range(nrb):
+        finish(i)
     flip(3)
 
     def colsum(ref):
@@ -697,10 +702,10 @@
             size = half * n
 
             def body(j):
-                v = dot(left[lhs, h * half:(h + 1) * half, :], rhs[:, at(j, BN)])
-                for t in range(BN // 128):
-                    stage[slot, pl.ds(2 * j + t, half, stride=n), :] = v[:, 128 * t:128 * (t + 1)]
-            loop(width // BN, body)
+                v = dot(left[lhs, h * half:(h + 1) * half, :], rhs[:, at(j, WN)])
+                for t in range(WN // 128):
+                    stage[slot, pl.ds(WN // 128 * j + t, half, stride=n), :] = v[:, 128 * t:128 * (t + 1)]
+            loop(width // WN, body)
             cp = pltpu.make_async_copy(stage.at[slot, 0:size, :], grad_hbm.at[first + h * size:first + (h + 1) * size, :], ssem.at[slot])
             cp.start()
             sent.append(cp)
@@ -711,20 +716,20 @@
     weight_grad(3, active, FF, row_out)
 
     def back_hidden(i):
-        v = dot(low[...], wo[:, at(i, BN)]) * slope[:, at(i, BN)]
+        v = dot(low[...], wo[:, at(i, GN)]) * slope[:, at(i, GN)]
         b = v.astype(BF16)
-        ghid[:, at(i, BN)] = b
+        ghid[:, at(i, GN)] = b
         s = jnp.sum(b.astype(F32), 0, keepdims=True)
-        for t in range(BN // 128):
-            vstage[pl.ds(bias_in_row + 2 * i + t, 1), :] = s[:, 128 * t:128 * (t + 1)]
-    loop(FF // BN, back_hidden)
+        for t in range(GN // 128):
+            vstage[pl.ds(bias_in_row + GN // 128 * i + t, 1), :] = s[:, 128 * t:128 * (t + 1)]
+    loop(FF // GN, back_hidden)
     weight_grad(2, ghid, FF, row_in)
 
     dnorm = igrad_ref
 
     def back_in(i):
-        dnorm[:, at(i, BN)] = dot_nt(ghid[...], wi[at(i, BN), :])
-    loop(D // BN, back_in)
+        dnorm[:, at(i, SN)] = dot_nt(ghid[...], wi[at(i, SN), :])
+    loop(D // SN, back_in)
 
     def norm_back(values, gain, dy):
         z, r = stats(values)
@@ -773,14 +778,14 @@
         gmix[rows, at(p + pairs, 128)] = (dot_tn(jnp.concatenate(out, axis=0), stack(q)) * scale).astype(BF16)
         pl_low = jnp.concatenate([pr[:, :128], pr[:, 128:]], axis=0).astype(BF16)
         gmix[rows, at(p + 2 * pairs, 128)] = dot_tn(pl_low, stack(do)).astype(BF16)
-    loop(pairs * (tokens // 128), attention_back)
+    several(pairs * (tokens // 128), attention_back)
     put_vector(2, colsum(gmix[:, 0:D]))
     put_vector(3, colsum(gmix[:, 2 * D:3 * D]))
     weight_grad(0, gmix, 3 * D, 0)
 
     def back_qkv(i):
-        dnorm[:, at(i, BN)] = dot_nt(gmix[...], wq[at(i, BN), :])
-    loop(D // BN, back_qkv)
+        dnorm[:, at(i, SN)] = dot_nt(gmix[...], wq[at(i, SN), :])
+    loop(D // SN, back_qkv)
     whole = rows_total
 
     def ln_one_back(i, carry):
@@ -828,25 +833,23 @@
     devices = lax.axis_size("dp") * lax.axis_size("fsdp")
     total_rows = params.shape[0] * devices
     used_rows = sum(h * w for h, w in MATS) // 128
-    mask_values = valid_mask.astype(jnp.float32)
-    count = jnp.full((8, 128), jnp.sum(mask_values))
+    mask = valid_mask.reshape(-1, 128)
     if custom:
-        *weights, vectors, count = gather(params, count, MATS, total_rows - used_rows)
+        *weights, vectors, count = gather(params, mask, MATS, total_rows - used_rows)
     else:
         whole = collect(params)
         weights = unpack(whole)[:4]
         vectors = whole[used_rows:].astype(jnp.float32)
-        count = lax.psum(count, ("dp", "fsdp"))
+        count = lax.psum(jnp.full((8, 128), jnp.sum(mask.astype(jnp.float32))), ("dp", "fsdp"))
     activations, input_grad, squares, grad = compute(
-        tokens, target, mask_values.reshape(-1, 1), vectors, count, weights, tokens.shape[0] * devices * D, total_rows
+        tokens, target, mask, vectors, count, weights, tokens.shape[0] * devices * D, total_rows
     )
     if custom:
-        gradient, squares = reduce(grad, squares, params.shape[0])
-        gradient = gradient[: params.shape[0]]
+        gradient, loss = reduce(grad, squares, count, params.shape[0])
+        gradient, loss = gradient[: params.shape[0]], loss.reshape(())
     else:
         gradient = reduce_rows(grad)
-        squares = lax.psum(squares, ("dp", "fsdp"))
-    loss = squares[0, 0] / (count[0, 0] * D)
+        loss = lax.psum(squares, ("dp", "fsdp"))[0, 0] / (count[0, 0] * D)
     new_first = beta_one * first_moment + (1.0 - beta_one) * gradient
     new_second = beta_two * second_moment + (1.0 - beta_two) * gradient * gradient
     first_hat = new_first / (1.0 - beta_one**STEP)

time: 254 us -> 207 us (0.81)
  Pallas kernels: 240 us -> 200 us
  local copies, waits for them, and re-layouts: 4.49 us -> 0 us
    pallas_call x1, Pallas kernels: 85.8 us -> 56 us  [compute(): pl.pallas_call(functools.partial(compute_kernel, float(whole)), out_shape...]
    pallas_call x1, Pallas kernels: 78.1 us -> 67.3 us  [reduce(): pl.pallas_call(functools.partial(reduce_kernel, parts, rows), out_shape=[...]
where the time goes in v1:
time: 207 us; the launch traced here: 206 us
  Pallas kernels  200 us (97%)
  other arithmetic  3.88 us (2%)
  between operations  2.4 us (1%)
    pallas_call x1, Pallas kernels, gather(): pl.pallas_call(functools.partial(gather_kernel, parts, rows, mats), out_s...  76.6 us
    pallas_call x1, Pallas kernels, reduce(): pl.pallas_call(functools.partial(reduce_kernel, parts, rows), out_shape=[...  67.3 us
    pallas_call x1, Pallas kernels, compute(): pl.pallas_call(functools.partial(compute_kernel, float(whole)), out_shape...  56 us

profile of v1, /device:TPU:0, one launch (start us, length us, event | category | flops | bytes accessed | tf_op | source)
XLA Modules:
  0.0 206.2 jit_solution(1240468636609645281)
XLA Ops:
  0.6 76.6 %gather_params.1 = (bf16[768,2304]{1,0:T(8,128)(2,1)}, bf16[768,768]{1,0:T(8,128)(2,1)}, bf16[768,3072]{1,0:T(8,128)(2,1)}, bf16[768,3072]{1,0:T(8,128)(2,1)}, f32[256,128]{1,0:T(8,128)}, /*index=5*/f32[8,128]{1,0:T(8,128)}) custom-call(f32[1736,128]{1,0:T(8,128)} %own_ref.1, s32[4,128]{1,0:T(4,128)} %bitcast.2), custom_call_target="tpu_custom_call" | custom-call | tf_op jit(solution)/shard_map/gather_params/pallas_call | solution.py:299
  77.2 56.0 %layer.1 = (bf16[512,768]{1,0:T(8,128)(2,1)}, f32[512,768]{1,0:T(8,128)}, f32[8,128]{1,0:T(8,128)}, f32[55552,128]{1,0:T(8,128)}) custom-call(bf16[512,768]{1,0:T(8,128)(2,1)} %x_ref.1, bf16[512,768]{1,0:T(8,128)(2,1)} %target_ref.1, s32[4,128]{1,0:T(4,128)} %bitcast.3, f32[256,128]{1,0:T(8,128)} %get-tuple-element.18.vec_ref, ...), custom_call_target="tpu_custom_call" | custom-call | tf_op jit(solution)/shard_map/layer/pallas_call | solution.py:811
  133.3 67.3 %reduce_gradient.1 = (f32[1744,128]{1,0:T(8,128)}, f32[1,1]{1,0:T(1,128)}) custom-call(f32[55552,128]{1,0:T(8,128)} %get-tuple-element.25.grad_ref, f32[8,128]{1,0:T(8,128)} %get-tuple-element.26.part_ref, f32[8,128]{1,0:T(8,128)} %get-tuple-element.19.count_ref), custom_call_target="tpu_custom_call" | custom-call | tf_op jit(solution)/shard_map/reduce_gradient/pallas_call | solution.py:492
  200.6 3.9 %multiply_subtract_fusion = (f32[1736,128]{1,0:T(8,128)}, f32[1736,128]{1,0:T(8,128)}, f32[1736,128]{1,0:T(8,128)}) fusion(f32[1736,128]{1,0:T(8,128)} %own_ref.1, f32[1744,128]{1,0:T(8,128)} %get-tuple-element.29, f32[1736,128]{1,0:T(8,128)} %param.10, f32[1736,128]{1,0:T(8,128)} %param.11), kind=kLoop, calls=%fused_computation.2 | loop fusion | flops 3333120 | bytes 6221824 | tf_op jit(solution)/shard_map/sub | solution.py:857

commit v2 on v1

--- a/solution.py
+++ b/solution.py
@@ -67,12 +67,12 @@
     return ((pos[0] * NB + pos[1]) * NX + pos[2]) * 2 + core
 
 
-def steps():
+def steps(later):
     out = []
     for da in range(-(NA - 1), NA):
         for db in range(2):
             for dx in range(2):
-                out.append((abs(da) + db + dx, (da, db, dx)))
+                out.append((abs(da) * 0.8 + db + dx + later(da, db, dx) * 0.01, (da, db, dx)))
     out.sort(key=lambda t: t[0])
     return [r for _, r in out]
 
@@ -152,7 +152,7 @@
     up, down = a + 1 < NA, a - 1 >= 0
     when(up, lambda: pl.semaphore_signal(sem, inc=1, device_id=device((a + 1, b, x), core), device_id_type=MESH))
     when(down, lambda: pl.semaphore_signal(sem, inc=1, device_id=device((a - 1, b, x), core), device_id_type=MESH))
-    pl.semaphore_wait(sem, len(fixed) + up.astype(jnp.int32) + down.astype(jnp.int32))
+    return lambda: pl.semaphore_wait(sem, len(fixed) + up.astype(jnp.int32) + down.astype(jnp.int32))
 
 
 class Total:
@@ -189,19 +189,15 @@
     mat_refs = refs[nm + 10:]
     pos, core = coords()
     me = flat(pos, core)
+    greeted = greet(pos, core)
     slots[me, 0:rows, :] = own_ref[...].astype(BF16)
     if slots.shape[1] > rows:
         slots[me, rows:, :] = jnp.zeros((slots.shape[1] - rows, 128), BF16)
     tbuf[0] = jnp.full(tbuf.shape[1:], jnp.sum(mask_ref[...].astype(F32)))
     total = Total(pos, core, tbuf, tsend, trecv)
-    greet(pos, core)
+    greeted()
     hooks = total.hooks(6, 14)
-    plan = steps()
-    order_k = []
-    for rel in plan:
-        for col in range(3):
-            order_k.append((rel, col))
-
+    plan = steps(lambda da, db, dx: (da < 0) == ((db + dx) % 2 == 0))
     def chunk(idx, col):
         lo, n = parts[col]
         return slots.at[idx, pl.ds(lo, n), :]
@@ -211,6 +207,11 @@
             src_ref=chunk(idx, col), dst_ref=chunk(idx, col),
             send_sem=send.at[k, direction], recv_sem=recv.at[idx, col],
             device_id=to, device_id_type=MESH)
+
+    def whole(idx, k):
+        return pltpu.make_async_remote_copy(
+            src_ref=slots.at[idx], dst_ref=slots.at[idx], send_sem=send.at[k, 4], recv_sem=recv.at[idx, 0],
+            device_id=device(pos, 1 - core), device_id_type=MESH)
 
     def widen(idx):
         base = pl.multiple_of(idx * rows, 8)
@@ -231,15 +232,15 @@
                 copy(idx, col, k, 0, device(pos, 1 - core)).wait_recv()
             for cond, child, direction in children(rel, ORDERS[col], pos):
                 when(cond, lambda child=child, direction=direction: copy(idx, col, k, direction, device(child, core)).start())
-            copy(idx, col, k, 4, device(pos, 1 - core)).start()
+            if col == 2:
+                whole(idx, k).start()
         when(valid, inner)
 
     def sibling(rel, k0):
         valid, src = source_of(rel, pos)
         def inner():
             other = flat(src, 1 - core)
-            for col in range(3):
-                copy(other, col, k0 + col, 4, device(pos, 1 - core)).wait_recv()
+            whole(other, k0 + 2).wait_recv()
             widen(flat(src, core))
             widen(other)
         when(valid, inner)
@@ -249,7 +250,8 @@
             idx = flat(src, core)
             for cond, child, direction in children(rel, ORDERS[col], pos):
                 when(cond, lambda child=child, direction=direction: copy(idx, col, k, direction, device(child, core)).wait_send())
-            copy(idx, col, k, 4, device(pos, 1 - core)).wait_send()
+            if col == 2:
+                whole(idx, k).wait_send()
         when(valid, inner)
 
     LAG = 2
@@ -265,20 +267,22 @@
     for i in range(len(plan) - LAG, len(plan)):
         sibling(plan[i], 3 * i)
     total_ref[...] = tbuf[2 * total.n]
-    first = 0
     copies = []
-    for (height, width), mat, out, s in zip(mats, mat_refs, outs, range(nm)):
+    starts = [sum(h * w for h, w in mats[:s]) // 128 for s in range(nm + 1)]
+    for s in sorted(range(nm), key=lambda s: -mats[s][0] * mats[s][1]):
+        (height, width), mat, first = mats[s], mat_refs[s], starts[s]
         n = width // 128
+
         def body(i, _, mat=mat, n=n, first=first):
             r = pl.multiple_of(i * 16, 16)
             for j in range(n):
                 mat[pl.ds(r, 16), 128 * j:128 * (j + 1)] = flat_ref[pl.ds(first + r * n + j, 16, stride=n), :].astype(BF16)
             return 0
         lax.fori_loop(0, height // 16, body, 0)
-        cp = pltpu.make_async_copy(mat, out, osem.at[s])
+        cp = pltpu.make_async_copy(mat, outs[s], osem.at[s])
         cp.start()
         copies.append(cp)
-        first += height * n
+    first = starts[nm]
     vec_ref[...] = flat_ref[first:first + vec_ref.shape[0], :]
     for i, rel in enumerate(plan):
         valid, src = source_of(rel, pos)
@@ -324,7 +328,7 @@
 def reduce_kernel(parts, rows, grad_ref, part_ref, count_ref, out_ref, loss_ref, part, rb_core, rb_x, rb_b, rb_a01, rb_a2, stage, acc,
                   ssem, send_c, recv_c, send_p, recv_x, recv_b, recv_a, tbuf, tsend, trecv):
     pos, core = coords()
-    plan = list(reversed(steps()))
+    plan = list(reversed(steps(lambda da, db, dx: da < 0)))
     depth = stage.shape[0]
     loads = []
     for rel in plan:
@@ -341,6 +345,7 @@
         valid, o, cp = load(i)
         when(valid, cp.start)
 
+    greeted = greet(pos, core)
     tbuf[0] = part_ref[...]
     for i in range(depth):
         start_load(i)
@@ -348,7 +353,7 @@
         for i in range(depth):
             stage[i, rows:, :] = jnp.zeros((stage.shape[1] - rows, 128), F32)
     total = Total(pos, core, tbuf, tsend, trecv)
-    greet(pos, core)
+    greeted()
     hooks = total.hooks(6, 14)
 
     def core_copy(rel):

time: 207 us -> 202 us (0.976)
  the two profiles are of different devices: /device:TPU:0 before, /device:TPU:17 now
where the time goes in v2:
time: 202 us; the launch traced here: 201 us
  Pallas kernels  195 us (97%)
  other arithmetic  3.88 us (2%)
  between operations  2.4 us (1%)
    pallas_call x1, Pallas kernels, gather(): pl.pallas_call(functools.partial(gather_kernel, parts, rows, mats), out_s...  70.1 us
    pallas_call x1, Pallas kernels, reduce(): pl.pallas_call(functools.partial(reduce_kernel, parts, rows), out_shape=[...  69.1 us
    pallas_call x1, Pallas kernels, compute(): pl.pallas_call(functools.partial(compute_kernel, float(whole)), out_shape...  56 us

profile of v2, /device:TPU:17, one launch (start us, length us, event | category | flops | bytes accessed | tf_op | source)
XLA Modules:
  0.0 201.4 jit_solution(11941255338525156798)
XLA Ops:
  0.6 70.1 %gather_params.1 = (bf16[768,2304]{1,0:T(8,128)(2,1)}, bf16[768,768]{1,0:T(8,128)(2,1)}, bf16[768,3072]{1,0:T(8,128)(2,1)}, bf16[768,3072]{1,0:T(8,128)(2,1)}, f32[256,128]{1,0:T(8,128)}, /*index=5*/f32[8,128]{1,0:T(8,128)}) custom-call(f32[1736,128]{1,0:T(8,128)} %own_ref.1, s32[4,128]{1,0:T(4,128)} %bitcast.2), custom_call_target="tpu_custom_call" | custom-call | tf_op jit(solution)/shard_map/gather_params/pallas_call | solution.py:303
  70.7 56.0 %layer.1 = (bf16[512,768]{1,0:T(8,128)(2,1)}, f32[512,768]{1,0:T(8,128)}, f32[8,128]{1,0:T(8,128)}, f32[55552,128]{1,0:T(8,128)}) custom-call(bf16[512,768]{1,0:T(8,128)(2,1)} %x_ref.1, bf16[512,768]{1,0:T(8,128)(2,1)} %target_ref.1, s32[4,128]{1,0:T(4,128)} %bitcast.3, f32[256,128]{1,0:T(8,128)} %get-tuple-element.18.vec_ref, ...), custom_call_target="tpu_custom_call" | custom-call | tf_op jit(solution)/shard_map/layer/pallas_call | solution.py:816
  126.7 69.1 %reduce_gradient.1 = (f32[1744,128]{1,0:T(8,128)}, f32[1,1]{1,0:T(1,128)}) custom-call(f32[55552,128]{1,0:T(8,128)} %get-tuple-element.25.grad_ref, f32[8,128]{1,0:T(8,128)} %get-tuple-element.26.part_ref, f32[8,128]{1,0:T(8,128)} %get-tuple-element.19.count_ref), custom_call_target="tpu_custom_call" | custom-call | tf_op jit(solution)/shard_map/reduce_gradient/pallas_call | solution.py:497
  195.8 3.9 %multiply_subtract_fusion = (f32[1736,128]{1,0:T(8,128)}, f32[1736,128]{1,0:T(8,128)}, f32[1736,128]{1,0:T(8,128)}) fusion(f32[1736,128]{1,0:T(8,128)} %own_ref.1, f32[1744,128]{1,0:T(8,128)} %get-tuple-element.29, f32[1736,128]{1,0:T(8,128)} %param.10, f32[1736,128]{1,0:T(8,128)} %param.11), kind=kLoop, calls=%fused_computation.2 | loop fusion | flops 3333120 | bytes 6221824 | tf_op jit(solution)/shard_map/sub | solution.py:862

commit v3 on v2

--- a/solution.py
+++ b/solution.py
@@ -574,7 +574,7 @@
         r = lax.rsqrt(jnp.mean(center * center, -1, keepdims=True) + norm_epsilon)
         return center * r, r
 
-    RB = 256
+    RB = 512
     nrb = tokens // RB
     low = glow
 
@@ -592,9 +592,9 @@
         c.start()
     BN = 256
     WN = 768
-    HN = 768
-    GN = 768
-    SN = 256
+    HN = 1536
+    GN = 1536
+    SN = 768
     QN = 768
     IN = 256
 
@@ -699,11 +699,11 @@
 
     def weight_grad(lhs, rhs, width, first):
         n = width // 128
-        half = D // 2
-        for h in range(2):
-            slot = len(sent) % 2
-            if len(sent) >= 2:
-                sent[-2].wait()
+        half = D
+        for h in range(1):
+            slot = 0
+            if sent:
+                sent[-1].wait()
             size = half * n
 
             def body(j):
@@ -801,7 +801,6 @@
     a, b = lax.fori_loop(0, nrb, ln_one_back, (zero, zero))
     put_vector(0, a)
     put_vector(1, b)
-    sent[-2].wait()
     sent[-1].wait()
     cp = pltpu.make_async_copy(vstage, grad_hbm.at[used_rows:used_rows + vstage.shape[0], :], ssem.at[0])
     cp.start()
@@ -824,7 +823,7 @@
             pltpu.VMEM((n, 3 * D), BF16), pltpu.VMEM((HEADS // 2 * (n // 128), 128, 256), F32), pltpu.VMEM((n, D), BF16),
             pltpu.VMEM((n, D), F32), pltpu.VMEM((n, FF), F32), pltpu.VMEM((n, FF), BF16), pltpu.VMEM((4, D, n), BF16),
             pltpu.VMEM((n, D), F32), pltpu.VMEM((n, D), BF16), pltpu.VMEM((n, FF), BF16), pltpu.VMEM((n, 3 * D), BF16),
-            pltpu.VMEM((2, D // 2 * FF // 128, 128), F32), pltpu.VMEM((total_rows - used_rows, 128), F32),
+            pltpu.VMEM((1, D * FF // 128, 128), F32), pltpu.VMEM((total_rows - used_rows, 128), F32),
             pltpu.SemaphoreType.DMA((4,)), pltpu.SemaphoreType.DMA((2,))],
         compiler_params=pltpu.CompilerParams(vmem_limit_bytes=67043328),
         name="layer",

time: 202 us -> 198 us (0.980)
  Pallas kernels: 195 us -> 191 us
    pallas_call x1, Pallas kernels: 56 us -> 52.1 us  [compute(): pl.pallas_call(functools.partial(compute_kernel, float(whole)), out_shape...]
where the time goes in v3:
time: 198 us
  Pallas kernels  191 us (96%)
  other arithmetic  3.88 us (2%)
  between operations  2.4 us (1%)
    pallas_call x1, Pallas kernels, gather(): pl.pallas_call(functools.partial(gather_kernel, parts, rows, mats), out_s...  70.1 us
    pallas_call x1, Pallas kernels, reduce(): pl.pallas_call(functools.partial(reduce_kernel, parts, rows), out_shape=[...  69.1 us
    pallas_call x1, Pallas kernels, compute(): pl.pallas_call(functools.partial(compute_kernel, float(whole)), out_shape...  52.1 us

profile of v3, /device:TPU:17, one launch (start us, length us, event | category | flops | bytes accessed | tf_op | source)
XLA Modules:
  0.0 197.5 jit_solution(1145671414009267750)
XLA Ops:
  0.6 70.1 %gather_params.1 = (bf16[768,2304]{1,0:T(8,128)(2,1)}, bf16[768,768]{1,0:T(8,128)(2,1)}, bf16[768,3072]{1,0:T(8,128)(2,1)}, bf16[768,3072]{1,0:T(8,128)(2,1)}, f32[256,128]{1,0:T(8,128)}, /*index=5*/f32[8,128]{1,0:T(8,128)}) custom-call(f32[1736,128]{1,0:T(8,128)} %own_ref.1, s32[4,128]{1,0:T(4,128)} %bitcast.2), custom_call_target="tpu_custom_call" | custom-call | tf_op jit(solution)/shard_map/gather_params/pallas_call | solution.py:303
  70.7 52.1 %layer.1 = (bf16[512,768]{1,0:T(8,128)(2,1)}, f32[512,768]{1,0:T(8,128)}, f32[8,128]{1,0:T(8,128)}, f32[55552,128]{1,0:T(8,128)}) custom-call(bf16[512,768]{1,0:T(8,128)(2,1)} %x_ref.1, bf16[512,768]{1,0:T(8,128)(2,1)} %target_ref.1, s32[4,128]{1,0:T(4,128)} %bitcast.3, f32[256,128]{1,0:T(8,128)} %get-tuple-element.18.vec_ref, ...), custom_call_target="tpu_custom_call" | custom-call | tf_op jit(solution)/shard_map/layer/pallas_call | solution.py:815
  122.8 69.1 %reduce_gradient.1 = (f32[1744,128]{1,0:T(8,128)}, f32[1,1]{1,0:T(1,128)}) custom-call(f32[55552,128]{1,0:T(8,128)} %get-tuple-element.25.grad_ref, f32[8,128]{1,0:T(8,128)} %get-tuple-element.26.part_ref, f32[8,128]{1,0:T(8,128)} %get-tuple-element.19.count_ref), custom_call_target="tpu_custom_call" | custom-call | tf_op jit(solution)/shard_map/reduce_gradient/pallas_call | solution.py:497
  191.9 3.9 %multiply_subtract_fusion = (f32[1736,128]{1,0:T(8,128)}, f32[1736,128]{1,0:T(8,128)}, f32[1736,128]{1,0:T(8,128)}) fusion(f32[1736,128]{1,0:T(8,128)} %own_ref.1, f32[1744,128]{1,0:T(8,128)} %get-tuple-element.29, f32[1736,128]{1,0:T(8,128)} %param.10, f32[1736,128]{1,0:T(8,128)} %param.11), kind=kLoop, calls=%fused_computation.2 | loop fusion | flops 3333120 | bytes 6221824 | tf_op jit(solution)/shard_map/sub | solution.py:861
